TPU v7x, 256 devices: a 4x2x16 block of a 4x16x16 slice. The times are simulated.
256 devices in a mesh: groups: 2 (over y), seq: 64 (over x, z), section: 2 (over core).
Axes of the slice: x: 4, y: 2, z: 16, core: 2. Of those that a mesh axis runs over, the one named last changes fastest.
The devices are a block of a 4x16x16 slice.
Arguments:
- hidden_in: bfloat16 [4, 8192], P('groups', 'seq'), parts along dimension 0, may hold values from -40 to 40
- norm_gain: bfloat16 [2, 8192], P('section', 'seq'), may hold values from 0.5 to 1.5
- qkv_weight: bfloat16 [2, 8192, 10240], P('section', 'seq'), as said below
- out_weight: bfloat16 [2, 8192, 8192], P('section', None, 'seq'), may hold values from -0.0625 to 0.0625
- memory: bfloat16 [2, 4, 8, 256, 2, 128, 128], P('section', 'groups', None, 'seq'), parts along dimension 1, may hold values from -12 to 12
- lengths: int32 [4], P('groups'), parts along dimension 0, may hold values from 16384 to 32768
- selected: int32 [4, 8, 16], P('groups'), parts along dimension 0, may hold values from 0 to 255, all different within a row
Outputs:
- hidden_out: bfloat16 [2, 4, 8192], P('section', 'groups', 'seq'), parts along dimension 1
- attention: bfloat16 [2, 4, 8192], P('section', 'groups'), parts along dimension 1
There are 2 independent parts, one for each index of `groups`. A program takes and returns all parts, laid end to end along the dimension named above; an argument that names none is the same for every part. Nothing has to cross between parts.
Inputs may be any that keep to these rules, and one draw needn't show every extreme that they name: `selected`: for each sequence and key-value head the 16 block numbers differ. `qkv_weight`: every entry's magnitude is at most 256 / sqrt(8192).
All inputs are finite; a program needn't handle non-finite values.
Results may differ from a plain program's by a relative error of at most 0.025.
The roundings to bfloat16 on the way count: a program that leaves them out, or rounds other values in their place, can miss the bound.
Values may be sent and summed in bfloat16 or wider, within the bound.
A program may use at most 128 MiB of HBM per device.

v0:
```python
import functools

import jax
import jax.numpy as jnp
from jax import lax
from jax.experimental import pallas as pl
from jax.experimental.pallas import tpu as pltpu
from jax.sharding import Mesh
from jax.sharding import PartitionSpec as P

MESH = pl.DeviceIdType.MESH
EPSILON = 1e-05
FLOOR = -1e30
RING_X = 4
PAIR_Z = 2
SEQ = ("seq_0", "seq_1")


def places(x_size):
    found = [(dx, dz) for dx in range(x_size) for dz in range(PAIR_Z)]
    hops = [min(dx, x_size - dx) + dz for dx, dz in found]
    return found, hops


def kernel(
    sizes,
    lengths,
    hidden_in,
    gain,
    selected,
    qkv_hbm,
    out_hbm,
    memory_hbm,
    hidden_out,
    attention_out,
    w_in,
    w_out,
    mem,
    live,
    hin,
    hnew,
    part,
    part_in,
    total,
    total_in,
    query,
    local,
    local_in,
    merged,
    merged_in,
    rows,
    own_rows,
    attended,
    fetch_sem,
    hop_sem,
    send,
    recv,
):
    seqs, heads_kv, group, head, block, blocks_local, x_size, z_size = sizes
    lanes = group * head
    q_width = heads_kv * lanes
    far_size = z_size // PAIR_Z
    offsets, hops = places(x_size)
    near_first = sorted(range(1, len(offsets)), key=lambda k: hops[k])
    far_first = near_first[::-1]
    ring_far = sorted(range(1, far_size), key=lambda k: -min(k, far_size - k))

    x = lax.axis_index(SEQ[0])
    z = lax.axis_index(SEQ[1])
    section = lax.axis_index("section")
    pair = lax.rem(z, PAIR_Z)
    base_z = z - pair
    shard = x * z_size + z
    scale = head ** (-0.5)

    fetch_in = pltpu.make_async_copy(qkv_hbm.at[0], w_in, fetch_sem.at[0])
    fetch_mem = pltpu.make_async_copy(memory_hbm.at[0], mem, fetch_sem.at[1])
    fetch_out = pltpu.make_async_copy(out_hbm.at[0], w_out, fetch_sem.at[2])
    fetch_in.start()
    fetch_mem.start()
    fetch_out.start()

    def in_block(k):
        dx, dz = offsets[k]
        return lax.rem(x + dx, x_size), lax.rem(pair + dz, PAIR_Z)

    def kv_of(k):
        bx, bz = in_block(k)
        return bx * PAIR_Z + bz

    def block_device(k):
        bx, bz = in_block(k)
        return {SEQ[0]: bx, SEQ[1]: base_z + bz}

    def far_device(k):
        return {SEQ[1]: lax.rem(z + k * PAIR_Z, z_size)}

    def opposite(k):
        dx, dz = offsets[k]
        return offsets.index(((x_size - dx) % x_size, dz))

    partner = {"section": 1 - section}
    barrier = pltpu.get_barrier_semaphore()
    for k in ring_far:
        pl.semaphore_signal(barrier, inc=1, device_id=far_device(k), device_id_type=MESH)
    for k in far_first:
        pl.semaphore_signal(barrier, inc=1, device_id=block_device(k), device_id_type=MESH)
    pl.semaphore_signal(barrier, inc=1, device_id=partner, device_id_type=MESH)

    tokens = blocks_local * block
    first_block = shard * blocks_local
    lane = lax.broadcasted_iota(jnp.int32, (heads_kv, tokens), 1)
    for b in range(seqs):
        chosen_ids = selected[b]
        lane_block = first_block + lane // block
        hit = jnp.zeros((heads_kv, tokens), jnp.float32)
        for s in range(selected.shape[2]):
            hit = jnp.where(chosen_ids[:, s : s + 1] == lane_block, 1.0, hit)
        hit = jnp.where(first_block * block + lane < lengths[b], hit, 0.0)
        for g in range(heads_kv):
            live[b, g] = jnp.broadcast_to(hit[g : g + 1, :], (group, tokens))

    pl.semaphore_wait(barrier, len(ring_far) + len(far_first) + 1)

    def copy_to(stage, k, slot, source, target, device):
        return pltpu.make_async_remote_copy(
            src_ref=source,
            dst_ref=target,
            send_sem=send.at[stage, k],
            recv_sem=recv.at[stage, slot],
            device_id=device,
            device_id_type=MESH,
        )

    pending = []

    def start(copy):
        copy.start()
        pending.append(copy)

    hop = pltpu.make_async_remote_copy(
        src_ref=hnew,
        dst_ref=hin,
        send_sem=hop_sem.at[0],
        recv_sem=hop_sem.at[1],
        device_id=partner,
        device_id_type=MESH,
    )

    @pl.when(section == 0)
    def _():
        hin[...] = hidden_in[...]

    fetch_in.wait()

    @pl.when(section == 1)
    def _():
        hop.wait_recv()

    wide = hin[...].astype(jnp.float32)
    normed = (wide * gain[...].astype(jnp.float32)).astype(jnp.bfloat16)
    squares = wide * wide
    for k in [*far_first, 0]:
        g = kv_of(k)
        at_q = pl.multiple_of(g * lanes, lanes)
        at_k = pl.multiple_of(q_width + g * head, head)
        at_v = pl.multiple_of(q_width + heads_kv * head + g * head, head)
        qs = jnp.dot(normed, w_in[:, pl.ds(at_q, lanes)], preferred_element_type=jnp.float32)
        ks = jnp.dot(normed, w_in[:, pl.ds(at_k, head)], preferred_element_type=jnp.float32)
        vs = jnp.dot(normed, w_in[:, pl.ds(at_v, head)], preferred_element_type=jnp.float32)
        for b in range(seqs):
            for r in range(group):
                part[k, b, r : r + 1, :] = qs[b : b + 1, r * head : (r + 1) * head]
        part[k, seqs, 0:2, :] = ks
        part[k, seqs, 2:4, :] = vs
        part[k, seqs, 4:6, :] = squares
        part[k, seqs, 6:8, :] = jnp.zeros((2, head), jnp.float32)
        if k:
            start(copy_to(0, k, k, part.at[k], part_in.at[k], block_device(k)))

    value = part[0]
    for k in near_first:
        copy_to(0, k, k, part.at[k], part_in.at[k], block_device(k)).wait_recv()
        value = value + part_in[k]
    total[...] = value
    for k in ring_far:
        start(copy_to(1, k, k, total, total_in.at[k], far_device(k)))
    for k in ring_far[::-1]:
        copy_to(1, k, k, total, total_in.at[k], far_device(k)).wait_recv()
        value = value + total_in[k]

    model_width = hin.shape[1] * x_size * z_size
    own_q, own_k, own_v = [], [], []
    for b in range(seqs):
        mean = jnp.sum(value[seqs, 4 + b : 5 + b, :], axis=1, keepdims=True) / model_width
        inverse = lax.rsqrt(mean + EPSILON)
        q = (value[b] * inverse).astype(jnp.bfloat16)
        query[0, b] = q
        own_q.append(q.astype(jnp.float32))
        own_k.append((value[seqs, b : b + 1, :] * inverse).astype(jnp.bfloat16).astype(jnp.float32))
        own_v.append(
            (value[seqs, 2 + b : 3 + b, :] * inverse).astype(jnp.bfloat16).astype(jnp.float32)
        )
    for k in far_first:
        slot = opposite(k)
        start(copy_to(2, k, slot, query.at[0], query.at[slot], block_device(k)))
    own_score = [
        jnp.sum(own_q[b] * own_k[b], axis=1, keepdims=True) * scale for b in range(seqs)
    ]

    fetch_mem.wait()
    stat_lane = lax.broadcasted_iota(jnp.int32, (group, head), 1)

    def attend(k):
        g = kv_of(k)
        peaks, sums = [], []
        for b in range(seqs):
            keys = mem[b, g, :, 0].reshape(tokens, head)
            values = mem[b, g, :, 1].reshape(tokens, head)
            mask = live[b, g] > 0.5
            score = lax.dot_general(
                query[k, b], keys, (((1,), (1,)), ((), ())), preferred_element_type=jnp.float32
            )
            score = jnp.where(mask, score * scale, FLOOR)
            peak = jnp.max(score, axis=1, keepdims=True)
            weight = jnp.where(mask, jnp.exp(score - peak), 0.0)
            high = weight.astype(jnp.bfloat16)
            low = (weight - high.astype(jnp.float32)).astype(jnp.bfloat16)
            both = jnp.concatenate([high, low], axis=0)
            mixed = jnp.dot(both, values, preferred_element_type=jnp.float32)
            local[k, b] = mixed[:group] + mixed[group:]
            peaks.append(peak)
            sums.append(jnp.sum(weight, axis=1, keepdims=True))
        stats = sums[1]
        stats = jnp.where(stat_lane < 3, sums[0], stats)
        stats = jnp.where(stat_lane < 2, peaks[1], stats)
        local[k, seqs] = jnp.where(stat_lane < 1, peaks[0], stats)

    attend(0)
    for k in near_first:
        slot = k
        copy_to(2, k, slot, query.at[0], query.at[slot], block_device(k)).wait_recv()
        attend(k)
        start(copy_to(3, k, k, local.at[k], local_in.at[k], block_device(k)))

    def combine(parts):
        top = parts[0][seqs]
        for p in parts[1:]:
            top = jnp.maximum(top, p[seqs])
        sums = jnp.zeros((group, head), jnp.float32)
        outs = [jnp.zeros((group, head), jnp.float32) for _ in range(seqs)]
        for p in parts:
            factor = jnp.where(stat_lane < 2, jnp.exp(jnp.minimum(p[seqs] - top, 0.0)), 0.0)
            wides = [
                jnp.broadcast_to(factor[:, b : b + 1], (group, head)) for b in range(seqs)
            ]
            sums = sums + p[seqs] * jnp.where(stat_lane < 3, wides[0], wides[1])
            outs = [outs[b] + p[b] * wides[b] for b in range(seqs)]
        return outs, jnp.where(stat_lane < 2, top, sums)

    for k in near_first:
        copy_to(3, k, k, local.at[k], local_in.at[k], block_device(k)).wait_recv()
    outs, stats = combine([local[0], *[local_in[k] for k in near_first]])
    for b in range(seqs):
        merged[b] = outs[b]
    merged[seqs] = stats
    for k in ring_far:
        start(copy_to(4, k, k, merged, merged_in.at[k], far_device(k)))
    for k in ring_far[::-1]:
        copy_to(4, k, k, merged, merged_in.at[k], far_device(k)).wait_recv()
    outs, stats = combine([merged[...], *[merged_in[k] for k in ring_far]])
    for b in range(seqs):
        peak, summed = stats[:, b : b + 1], stats[:, 2 + b : 3 + b]
        top = jnp.maximum(peak, own_score[b])
        old, own = jnp.exp(peak - top), jnp.exp(own_score[b] - top)
        result = (outs[b] * old + own * own_v[b]) / (summed * old + own)
        for r in range(group):
            rows[b : b + 1, r * head : (r + 1) * head] = result[r : r + 1, :]
    own_g = kv_of(0)
    own_rows[...] = rows[...].astype(jnp.bfloat16)
    for k in far_first:
        slot = opposite(k)
        start(copy_to(5, k, slot, own_rows, attended.at[slot], block_device(k)))

    fetch_out.wait()
    branch = jnp.dot(
        own_rows[...],
        w_out[pl.ds(pl.multiple_of(own_g * lanes, lanes), lanes), :],
        preferred_element_type=jnp.float32,
    )
    attention_out[0, :, pl.ds(pl.multiple_of(own_g * lanes, lanes), lanes)] = own_rows[...]
    for k in near_first:
        copy_to(5, k, k, own_rows, attended.at[k], block_device(k)).wait_recv()
        at = pl.multiple_of(kv_of(k) * lanes, lanes)
        piece = attended[k]
        branch = branch + jnp.dot(
            piece, w_out[pl.ds(at, lanes), :], preferred_element_type=jnp.float32
        )
        attention_out[0, :, pl.ds(at, lanes)] = piece
    new = (wide + branch).astype(jnp.bfloat16)
    hidden_out[0] = new

    @pl.when(section == 0)
    def _():
        hnew[...] = new
        hop.start()
        hop.wait_send()

    for copy in pending:
        copy.wait_send()


def body(hidden_in, norm_gain, qkv_weight, out_weight, memory, lengths, selected):
    seqs, width = hidden_in.shape
    _, _, heads_kv, blocks_local, _, block, head = memory.shape
    heads_total = out_weight.shape[1]
    group = heads_total // (heads_kv * head)
    x_size, z_size = lax.axis_size(SEQ[0]), lax.axis_size(SEQ[1])
    sizes = (seqs, heads_kv, group, head, block, blocks_local, x_size, z_size)
    members = x_size * PAIR_Z
    far = z_size // PAIR_Z
    tile = (seqs + 1, group, head)
    f32, bf16 = jnp.float32, jnp.bfloat16
    vmem = pl.BlockSpec(memory_space=pltpu.VMEM)
    hbm = pl.BlockSpec(memory_space=pl.ANY)
    slots = max(members, far)
    return pl.pallas_call(
        functools.partial(kernel, sizes),
        out_shape=(
            jax.ShapeDtypeStruct((1, seqs, width), bf16),
            jax.ShapeDtypeStruct((1, seqs, heads_total), bf16),
        ),
        in_specs=[pl.BlockSpec(memory_space=pltpu.SMEM), vmem, vmem, vmem, hbm, hbm, hbm],
        out_specs=(vmem, vmem),
        scratch_shapes=[
            pltpu.VMEM(qkv_weight.shape[1:], bf16),
            pltpu.VMEM(out_weight.shape[1:], bf16),
            pltpu.VMEM(memory.shape[1:], bf16),
            pltpu.VMEM((seqs, heads_kv, group, blocks_local * block), f32),
            pltpu.VMEM((seqs, width), bf16),
            pltpu.VMEM((seqs, width), bf16),
            pltpu.VMEM((members, *tile), f32),
            pltpu.VMEM((members, *tile), f32),
            pltpu.VMEM(tile, f32),
            pltpu.VMEM((far, *tile), f32),
            pltpu.VMEM((members, seqs, group, head), bf16),
            pltpu.VMEM((members, *tile), f32),
            pltpu.VMEM((members, *tile), f32),
            pltpu.VMEM(tile, f32),
            pltpu.VMEM((far, *tile), f32),
            pltpu.VMEM((seqs, group * head), f32),
            pltpu.VMEM((seqs, group * head), bf16),
            pltpu.VMEM((members, seqs, group * head), bf16),
            pltpu.SemaphoreType.DMA((3,)),
            pltpu.SemaphoreType.DMA((2,)),
            pltpu.SemaphoreType.DMA((6, slots)),
            pltpu.SemaphoreType.DMA((6, slots)),
        ],
        compiler_params=pltpu.CompilerParams(collective_id=0, has_side_effects=True),
        name="decode",
    )(lengths, hidden_in, norm_gain, selected, qkv_weight, out_weight, memory)


def solution(mesh):
    z_size = mesh.shape["seq"] // RING_X
    finer = Mesh(
        mesh.devices.reshape(mesh.shape["groups"], RING_X, z_size, mesh.shape["section"]),
        ("groups", *SEQ, "section"),
    )
    in_specs = (
        P("groups", SEQ),
        P("section", SEQ),
        P("section", SEQ, None),
        P("section", None, SEQ),
        P("section", "groups", None, SEQ, None, None, None),
        P("groups"),
        P("groups", None, None),
    )
    out_specs = (P("section", "groups", SEQ), P("section", "groups", None))
    return jax.shard_map(body, mesh=finer, in_specs=in_specs, out_specs=out_specs, check_vma=False)
```

profile of v0, /device:TPU:33, one launch (start us, length us, event | category | flops | bytes accessed | tf_op | source)
XLA Modules:
  0.0 98.7 jit_solution(12592247861855559027)
XLA Ops:
  0.6 95.4 %decode.1 = (bf16[1,2,128]{2,1,0:T(2,128)(2,1)}, bf16[1,2,8192]{2,1,0:T(2,128)(2,1)}) custom-call(s32[2]{0:T(128)} %lengths.1, bf16[2,128]{1,0:T(2,128)(2,1)} %hidden_in.1, bf16[1,128]{1,0:T(2,128)(2,1)} %gain.1, s32[2,8,16]{2,1,0:T(8,128)} %selected.1, bf16[1,128,10240]{2,1,0:T(8,128)(2,1)} %qkv_hbm.1, bf16[1,8192,128]{2,1,0:T(8,128)(2,1)} %out_hbm.1, ...), custom_call_target="tpu_custom_call" | custom-call | tf_op jit(solution)/shard_map/decode/pallas_call | solution.py:327
  96.1 1.2 %copy.11 = bf16[1,2,128]{2,1,0:T(2,128)(2,1)} copy(bf16[1,2,128]{2,1,0:T(2,128)(2,1)} %get-tuple-element.4) | data formatting | bytes 1024
  97.3 1.4 %copy.12 = bf16[1,2,8192]{2,1,0:T(2,128)(2,1)} copy(bf16[1,2,8192]{2,1,0:T(2,128)(2,1)} %get-tuple-element.5) | data formatting | bytes 65536
where the time goes:
time: 98.9 us; the launch traced here: 98.7 us
  Pallas kernels  95.4 us (96%)
  local copies, waits for them, and re-layouts  2.57 us (3%)
    pallas_call x1, Pallas kernels, body(): pl.pallas_call(functools.partial(kernel, sizes), out_shape=(jax.ShapeDtyp...  95.4 us
    unnamed x2, local copies, waits for them, and re-layouts  2.57 us

commit v1 on v0

v1 whole, which is shorter than its diff:
```python
import functools

import jax
import jax.numpy as jnp
from jax import lax
from jax.experimental import pallas as pl
from jax.experimental.pallas import tpu as pltpu
from jax.sharding import Mesh
from jax.sharding import PartitionSpec as P

MESH = pl.DeviceIdType.MESH
EPSILON = 1e-05
FLOOR = -1e30
RING_X = 4
PAIR_Z = 2
SEQ = ("seq_0", "seq_1")
F32, BF16 = jnp.float32, jnp.bfloat16


def kernel(
    sizes,
    lengths_hbm,
    hidden_hbm,
    gain_hbm,
    selected_hbm,
    qkv_hbm,
    out_hbm,
    memory_hbm,
    result,
    lengths,
    selected,
    gain,
    hin,
    w_in,
    w_out,
    w_out_near,
    mem,
    mem_near,
    live,
    part,
    part_in,
    total,
    total_in,
    query,
    local,
    local_in,
    merged,
    merged_in,
    rows,
    own_rows,
    attended,
    done,
    done_in,
    fetch_sem,
    cast_sem,
    send,
    recv,
):
    seqs, heads_kv, group, head, block, blocks_local, x_size, z_size = sizes
    lanes = group * head
    q_width = heads_kv * lanes
    kv_width = heads_kv * head
    tokens = blocks_local * block
    far_size = z_size // PAIR_Z
    offsets = [(dx, dz) for dx in range(x_size) for dz in range(PAIR_Z)]
    hops = [min(dx, x_size - dx) + dz for dx, dz in offsets]
    near_first = sorted(range(1, len(offsets)), key=lambda k: hops[k])
    far_first = near_first[::-1]
    ring_far = sorted(range(1, far_size), key=lambda k: -min(k, far_size - k))

    x = lax.axis_index(SEQ[0])
    z = lax.axis_index(SEQ[1])
    section = lax.axis_index("section")
    pair = lax.rem(z, PAIR_Z)
    base_z = z - pair
    first_block = (x * z_size + z) * blocks_local
    scale = head ** (-0.5)
    model_width = hin.shape[2] * x_size * z_size

    def in_block(k):
        dx, dz = offsets[k]
        return lax.rem(x + dx, x_size), lax.rem(pair + dz, PAIR_Z)

    def kv_of(k):
        bx, bz = in_block(k)
        return bx * PAIR_Z + bz

    def block_device(k, core):
        bx, bz = in_block(k)
        return {SEQ[0]: bx, SEQ[1]: base_z + bz, "section": core}

    def far_device(k):
        return {SEQ[1]: lax.rem(z + k * PAIR_Z, z_size)}

    def opposite(k):
        dx, dz = offsets[k]
        return offsets.index(((x_size - dx) % x_size, dz))

    barrier = pltpu.get_barrier_semaphore()

    def greet(device):
        pl.semaphore_signal(barrier, inc=1, device_id=device, device_id_type=MESH)

    def copy_to(stage, k, slot, source, target, device):
        return pltpu.make_async_remote_copy(
            src_ref=source,
            dst_ref=target,
            send_sem=send.at[stage, k],
            recv_sem=recv.at[stage, slot],
            device_id=device,
            device_id_type=MESH,
        )

    def cast(number, source, target, core):
        return pltpu.make_async_remote_copy(
            src_ref=source,
            dst_ref=target,
            send_sem=cast_sem.at[0, number],
            recv_sem=cast_sem.at[1, number],
            device_id={"section": core},
            device_id_type=MESH,
        )

    cast_hidden = cast(0, hidden_hbm, hin.at[1], 1)
    cast_mem = cast(1, memory_hbm.at[0], mem_near, 1)
    cast_out = cast(2, out_hbm.at[0], w_out_near, 1)
    cast_done = cast(3, done, done_in, 0)

    fetch_gain = pltpu.make_async_copy(gain_hbm, gain, fetch_sem.at[0])
    fetch_hidden = pltpu.make_async_copy(hidden_hbm, hin.at[0], fetch_sem.at[1])
    fetch_kv = pltpu.make_async_copy(
        qkv_hbm.at[0, :, pl.ds(q_width, 2 * kv_width)],
        w_in.at[:, pl.ds(q_width, 2 * kv_width)],
        fetch_sem.at[2],
    )

    def q_columns(k):
        return pl.ds(pl.multiple_of(kv_of(k) * lanes, lanes), lanes)

    def fetch_q(k):
        return pltpu.make_async_copy(
            qkv_hbm.at[0, :, q_columns(k)], w_in.at[:, q_columns(k)], fetch_sem.at[8 + k]
        )

    fetch_selected = pltpu.make_async_copy(selected_hbm, selected, fetch_sem.at[3])
    fetch_lengths = pltpu.make_async_copy(lengths_hbm, lengths, fetch_sem.at[4])
    fetch_mem = pltpu.make_async_copy(memory_hbm.at[0], mem, fetch_sem.at[5])
    fetch_out = pltpu.make_async_copy(out_hbm.at[0], w_out, fetch_sem.at[6])

    @pl.when(section == 0)
    def _():
        greet({"section": 1})

    @pl.when(section == 1)
    def _():
        for k in [*far_first, 0]:
            greet(block_device(k, 0))
        for k in ring_far:
            greet(far_device(k))
        for k in far_first:
            greet(block_device(k, 1))

    fetch_gain.start()

    @pl.when(section == 0)
    def _():
        fetch_hidden.start()

    fetch_kv.start()
    for k in [*far_first, 0]:
        fetch_q(k).start()

    def project(wide, ready, send_one):
        normed = (wide * gain[...].astype(F32)).astype(BF16)
        squares = wide * wide
        for k in [*far_first, 0]:
            g = kv_of(k)
            at_k = pl.multiple_of(q_width + g * head, head)
            at_v = pl.multiple_of(q_width + kv_width + g * head, head)
            ready(k)
            qs = jnp.dot(normed, w_in[:, q_columns(k)], preferred_element_type=F32)
            ks = jnp.dot(normed, w_in[:, pl.ds(at_k, head)], preferred_element_type=F32)
            vs = jnp.dot(normed, w_in[:, pl.ds(at_v, head)], preferred_element_type=F32)
            for b in range(seqs):
                for r in range(group):
                    part[k, b, r : r + 1, :] = qs[b : b + 1, r * head : (r + 1) * head]
            part[k, seqs, 0:2, :] = ks
            part[k, seqs, 2:4, :] = vs
            part[k, seqs, 4:6, :] = squares
            part[k, seqs, 6:8, :] = jnp.zeros((2, head), F32)
            send_one(k)

    @pl.when(section == 0)
    def _():
        fetch_gain.wait()
        fetch_hidden.wait()
        fetch_kv.wait()
        sent = []

        def send_one(k):
            if not sent:
                pl.semaphore_wait(barrier, len(offsets))
            copy = copy_to(0, k, k, part.at[k], part_in.at[0, k], block_device(k, 1))
            copy.start()
            sent.append(copy)

        project(hin[0].astype(F32), lambda k: fetch_q(k).wait(), send_one)
        cast_hidden.start()
        cast_mem.start()
        cast_out.start()
        for copy in [*sent, cast_hidden, cast_mem, cast_out]:
            copy.wait_send()
        cast_done.wait_recv()
        result[0] = done_in[...]

    @pl.when(section == 1)
    def _():
        fetch_selected.start()
        fetch_lengths.start()
        fetch_mem.start()
        fetch_out.start()

        fetch_selected.wait()
        fetch_lengths.wait()
        lane = lax.broadcasted_iota(jnp.int32, (heads_kv, tokens), 1)
        for b in range(seqs):
            chosen_ids = selected[b]
            lane_block = first_block + lane // block
            hit = jnp.zeros((heads_kv, tokens), F32)
            for s in range(selected.shape[2]):
                hit = jnp.where(chosen_ids[:, s : s + 1] == lane_block, 1.0, hit)
            hit = jnp.where(first_block * block + lane < lengths[b], hit, 0.0)
            for g in range(heads_kv):
                live[b, g] = jnp.broadcast_to(hit[g : g + 1, :], (group, tokens))
        stat_lane = lax.broadcasted_iota(jnp.int32, (group, head), 1)
        pending = []

        def start(copy):
            copy.start()
            pending.append(copy)

        def attend(layer, k, memory):
            g = kv_of(k)
            peaks, sums = [], []
            for b in range(seqs):
                keys = memory[b, g, :, 0].reshape(tokens, head)
                values = memory[b, g, :, 1].reshape(tokens, head)
                mask = live[b, g] > 0.5
                score = lax.dot_general(
                    query[layer, k, b], keys, (((1,), (1,)), ((), ())), preferred_element_type=F32
                )
                score = jnp.where(mask, score * scale, FLOOR)
                peak = jnp.max(score, axis=1, keepdims=True)
                weight = jnp.where(mask, jnp.exp(score - peak), 0.0)
                high = weight.astype(BF16)
                low = (weight - high.astype(F32)).astype(BF16)
                both = jnp.concatenate([high, low], axis=0)
                mixed = jnp.dot(both, values, preferred_element_type=F32)
                local[layer, k, b] = mixed[:group] + mixed[group:]
                peaks.append(peak)
                sums.append(jnp.sum(weight, axis=1, keepdims=True))
            stats = sums[1]
            stats = jnp.where(stat_lane < 3, sums[0], stats)
            stats = jnp.where(stat_lane < 2, peaks[1], stats)
            local[layer, k, seqs] = jnp.where(stat_lane < 1, peaks[0], stats)

        def combine(parts):
            top = parts[0][seqs]
            for p in parts[1:]:
                top = jnp.maximum(top, p[seqs])
            sums = jnp.zeros((group, head), F32)
            outs = [jnp.zeros((group, head), F32) for _ in range(seqs)]
            for p in parts:
                factor = jnp.where(stat_lane < 2, jnp.exp(jnp.minimum(p[seqs] - top, 0.0)), 0.0)
                wides = [
                    jnp.broadcast_to(factor[:, b : b + 1], (group, head)) for b in range(seqs)
                ]
                sums = sums + p[seqs] * jnp.where(stat_lane < 3, wides[0], wides[1])
                outs = [outs[b] + p[b] * wides[b] for b in range(seqs)]
            return outs, jnp.where(stat_lane < 2, top, sums)

        def after_projection(layer, value, wide_of, memory, memory_ready, weights, weights_ready):
            stage = 6 * layer
            total[layer] = value
            if layer == 0:
                pl.semaphore_wait(barrier, len(ring_far) + len(far_first) + 1)

            def far_copy(n, k, source, target):
                return copy_to(stage + n, k, k, source, target, far_device(k))

            def block_copy(n, k, slot, source, target):
                return copy_to(stage + n, k, slot, source, target, block_device(k, 1))

            for k in ring_far:
                start(far_copy(1, k, total.at[layer], total_in.at[layer, k]))
            for k in ring_far[::-1]:
                far_copy(1, k, total.at[layer], total_in.at[layer, k]).wait_recv()
                value = value + total_in[layer, k]

            own_q, own_k, own_v = [], [], []
            for b in range(seqs):
                mean = jnp.sum(value[seqs, 4 + b : 5 + b, :], axis=1, keepdims=True) / model_width
                inverse = lax.rsqrt(mean + EPSILON)
                q = (value[b] * inverse).astype(BF16)
                query[layer, 0, b] = q
                own_q.append(q.astype(F32))
                own_k.append((value[seqs, b : b + 1, :] * inverse).astype(BF16).astype(F32))
                own_v.append((value[seqs, 2 + b : 3 + b, :] * inverse).astype(BF16).astype(F32))
            for k in far_first:
                slot = opposite(k)
                start(block_copy(2, k, slot, query.at[layer, 0], query.at[layer, slot]))
            own_score = [
                jnp.sum(own_q[b] * own_k[b], axis=1, keepdims=True) * scale for b in range(seqs)
            ]

            memory_ready()
            attend(layer, 0, memory)
            for k in near_first:
                block_copy(2, k, k, query.at[layer, 0], query.at[layer, k]).wait_recv()
                attend(layer, k, memory)
                start(block_copy(3, k, k, local.at[layer, k], local_in.at[layer, k]))
            for k in near_first:
                block_copy(3, k, k, local.at[layer, k], local_in.at[layer, k]).wait_recv()
            outs, stats = combine([local[layer, 0], *[local_in[layer, k] for k in near_first]])
            for b in range(seqs):
                merged[layer, b] = outs[b]
            merged[layer, seqs] = stats
            for k in ring_far:
                start(far_copy(4, k, merged.at[layer], merged_in.at[layer, k]))
            for k in ring_far[::-1]:
                far_copy(4, k, merged.at[layer], merged_in.at[layer, k]).wait_recv()
            outs, stats = combine([merged[layer], *[merged_in[layer, k] for k in ring_far]])
            for b in range(seqs):
                peak, summed = stats[:, b : b + 1], stats[:, 2 + b : 3 + b]
                top = jnp.maximum(peak, own_score[b])
                old, own = jnp.exp(peak - top), jnp.exp(own_score[b] - top)
                shared = (outs[b] * old + own * own_v[b]) / (summed * old + own)
                for r in range(group):
                    rows[b : b + 1, r * head : (r + 1) * head] = shared[r : r + 1, :]
            own_rows[layer] = rows[...].astype(BF16)
            for k in far_first:
                slot = opposite(k)
                start(block_copy(5, k, slot, own_rows.at[layer], attended.at[layer, slot]))

            weights_ready()
            branch = jnp.zeros((seqs, done.shape[1] - q_width), F32)
            for k in [0, *near_first]:
                if k:
                    block_copy(5, k, k, own_rows.at[layer], attended.at[layer, k]).wait_recv()
                piece = attended[layer, k] if k else own_rows[layer]
                branch = branch + jnp.dot(
                    piece, weights[q_columns(k), :], preferred_element_type=F32
                )
                if layer == 0:
                    done[:, q_columns(k)] = piece
                else:
                    result[0, :, q_columns(k)] = piece
            return (wide_of() + branch).astype(BF16)

        value = None
        for k in [0, *near_first]:
            copy_to(0, k, k, part.at[k], part_in.at[0, k], block_device(k, 1)).wait_recv()
            value = part_in[0, k] if value is None else value + part_in[0, k]

        def first_hidden():
            cast_hidden.wait_recv()
            return hin[1].astype(F32)

        new = after_projection(
            0, value, first_hidden, mem_near, cast_mem.wait_recv, w_out_near, cast_out.wait_recv
        )
        done[:, q_width:] = new
        fetch_gain.wait()
        fetch_kv.wait()
        for k in [*far_first, 0]:
            fetch_q(k).wait()
        wide = new.astype(F32)

        def send_one(k):
            if k:
                start(copy_to(6, k, k, part.at[k], part_in.at[1, k], block_device(k, 1)))

        project(wide, lambda k: None, send_one)
        start(cast_done)
        value = part[0]
        for k in near_first:
            copy_to(6, k, k, part.at[k], part_in.at[1, k], block_device(k, 1)).wait_recv()
            value = value + part_in[1, k]
        new = after_projection(1, value, lambda: wide, mem, fetch_mem.wait, w_out, fetch_out.wait)
        result[0, :, q_width:] = new
        for copy in pending:
            copy.wait_send()


def body(hidden_in, norm_gain, qkv_weight, out_weight, memory, lengths, selected):
    seqs, width = hidden_in.shape
    _, _, heads_kv, blocks_local, _, block, head = memory.shape
    heads_total = out_weight.shape[1]
    group = heads_total // (heads_kv * head)
    x_size, z_size = lax.axis_size(SEQ[0]), lax.axis_size(SEQ[1])
    sizes = (seqs, heads_kv, group, head, block, blocks_local, x_size, z_size)
    members = x_size * PAIR_Z
    far = z_size // PAIR_Z
    tile = (seqs + 1, group, head)
    hbm = pl.BlockSpec(memory_space=pl.ANY)
    slots = max(members, far)
    result = pl.pallas_call(
        functools.partial(kernel, sizes),
        out_shape=jax.ShapeDtypeStruct((1, seqs, heads_total + width), BF16),
        in_specs=[hbm] * 7,
        out_specs=pl.BlockSpec(memory_space=pltpu.VMEM),
        scratch_shapes=[
            pltpu.SMEM(lengths.shape, jnp.int32),
            pltpu.VMEM(selected.shape, jnp.int32),
            pltpu.VMEM((1, width), BF16),
            pltpu.VMEM((2, seqs, width), BF16),
            pltpu.VMEM(qkv_weight.shape[1:], BF16),
            pltpu.VMEM(out_weight.shape[1:], BF16),
            pltpu.VMEM(out_weight.shape[1:], BF16),
            pltpu.VMEM(memory.shape[1:], BF16),
            pltpu.VMEM(memory.shape[1:], BF16),
            pltpu.VMEM((seqs, heads_kv, group, blocks_local * block), F32),
            pltpu.VMEM((members, *tile), F32),
            pltpu.VMEM((2, members, *tile), F32),
            pltpu.VMEM((2, *tile), F32),
            pltpu.VMEM((2, far, *tile), F32),
            pltpu.VMEM((2, members, seqs, group, head), BF16),
            pltpu.VMEM((2, members, *tile), F32),
            pltpu.VMEM((2, members, *tile), F32),
            pltpu.VMEM((2, *tile), F32),
            pltpu.VMEM((2, far, *tile), F32),
            pltpu.VMEM((seqs, group * head), F32),
            pltpu.VMEM((2, seqs, group * head), BF16),
            pltpu.VMEM((2, members, seqs, group * head), BF16),
            pltpu.VMEM((seqs, heads_total + width), BF16),
            pltpu.VMEM((seqs, heads_total + width), BF16),
            pltpu.SemaphoreType.DMA((8 + members,)),
            pltpu.SemaphoreType.DMA((2, 4)),
            pltpu.SemaphoreType.DMA((12, slots)),
            pltpu.SemaphoreType.DMA((12, slots)),
        ],
        compiler_params=pltpu.CompilerParams(collective_id=0, has_side_effects=True),
        name="decode",
    )(lengths, hidden_in, norm_gain, selected, qkv_weight, out_weight, memory)
    return result[:, :, heads_total:], result[:, :, :heads_total]


def solution(mesh):
    z_size = mesh.shape["seq"] // RING_X
    finer = Mesh(
        mesh.devices.reshape(mesh.shape["groups"], RING_X, z_size, mesh.shape["section"]),
        ("groups", *SEQ, "section"),
    )
    in_specs = (
        P("groups", SEQ),
        P("section", SEQ),
        P("section", SEQ, None),
        P("section", None, SEQ),
        P("section", "groups", None, SEQ, None, None, None),
        P("groups"),
        P("groups", None, None),
    )
    out_specs = (P("section", "groups", SEQ), P("section", "groups", None))
    return jax.shard_map(body, mesh=finer, in_specs=in_specs, out_specs=out_specs, check_vma=False)
```

time: 98.9 us -> 89.5 us (0.905)
  Pallas kernels: 95.4 us -> 86.2 us
    pallas_call x1, Pallas kernels: 95.4 us -> 86.2 us  [body(): pl.pallas_call(functools.partial(kernel, sizes), out_shape=jax.ShapeDtype...]
    unnamed x2 -> x0, local copies, waits for them, and re-layouts: 2.57 us -> none
    slice x0 -> x2, local copies, waits for them, and re-layouts: none -> 2.53 us  [body(): return (result[:, :, heads_total:], result[:, :, :heads_total])]
where the time goes in v1:
time: 89.5 us; the launch traced here: 89.3 us
  Pallas kernels  86.2 us (96%)
  local copies, waits for them, and re-layouts  2.53 us (3%)
    pallas_call x1, Pallas kernels, body(): pl.pallas_call(functools.partial(kernel, sizes), out_shape=jax.ShapeDtype...  86.2 us
    slice x2, local copies, waits for them, and re-layouts, body(): return (result[:, :, heads_total:], result[:, :, :heads_total])  2.53 us

profile of v1, /device:TPU:33, one launch (start us, length us, event | category | flops | bytes accessed | tf_op | source)
XLA Modules:
  0.0 89.3 jit_solution(9493387292727007709)
XLA Ops:
  0.6 86.2 %decode.1 = bf16[1,2,8320]{2,1,0:T(2,128)(2,1)} custom-call(s32[2]{0:T(128)} %lengths_hbm.1, bf16[2,128]{1,0:T(2,128)(2,1)} %hidden_hbm.1, bf16[1,128]{1,0:T(2,128)(2,1)} %gain_hbm.1, s32[2,8,16]{2,1,0:T(8,128)} %selected_hbm.1, bf16[1,128,10240]{2,1,0:T(8,128)(2,1)} %qkv_hbm.1, bf16[1,8192,128]{2,1,0:T(8,128)(2,1)} %out_hbm.1, ...), custom_call_target="tpu_custom_call" | custom-call | tf_op jit(solution)/shard_map/decode/pallas_call | solution.py:407
  86.8 1.1 %slice.6 = bf16[1,2,128]{2,1,0:T(2,128)(2,1)} slice(bf16[1,2,8320]{2,1,0:T(2,128)(2,1)} %decode.1), slice={[0:1], [0:2], [8192:8320]} | slice | bytes 1024 | tf_op jit(solution)/shard_map/slice | solution.py:445
  87.9 1.4 %slice.7 = bf16[1,2,8192]{2,1,0:T(2,128)(2,1)} slice(bf16[1,2,8320]{2,1,0:T(2,128)(2,1)} %decode.1), slice={[0:1], [0:2], [0:8192]} | slice | bytes 65536 | tf_op jit(solution)/shard_map/slice | solution.py:445

commit v2 on v1

--- a/solution.py
+++ b/solution.py
@@ -15,6 +15,7 @@
 PAIR_Z = 2
 SEQ = ("seq_0", "seq_1")
 F32, BF16 = jnp.float32, jnp.bfloat16
+VMEM_BYTES = 64000000
 
 
 def kernel(
@@ -34,9 +35,11 @@
     w_in,
     w_out,
     w_out_near,
-    mem,
+    mem_stage,
+    mem_block,
     mem_near,
     live,
+    live_block,
     part,
     part_in,
     total,
@@ -53,6 +56,8 @@
     done_in,
     fetch_sem,
     cast_sem,
+    ready_sem,
+    group_sem,
     send,
     recv,
 ):
@@ -121,6 +126,26 @@
             device_id_type=MESH,
         )
 
+    def stage_memory(k):
+        return pltpu.make_async_remote_copy(
+            src_ref=memory_hbm.at[0, :, kv_of(k)],
+            dst_ref=mem_stage.at[k],
+            send_sem=group_sem.at[0, k],
+            recv_sem=group_sem.at[1, k],
+            device_id={"section": 0},
+            device_id_type=MESH,
+        )
+
+    def regroup(k, slot):
+        return pltpu.make_async_remote_copy(
+            src_ref=mem_stage.at[k],
+            dst_ref=mem_block.at[slot],
+            send_sem=group_sem.at[2, k],
+            recv_sem=group_sem.at[3, slot],
+            device_id=block_device(k, 1),
+            device_id_type=MESH,
+        )
+
     cast_hidden = cast(0, hidden_hbm, hin.at[1], 1)
     cast_mem = cast(1, memory_hbm.at[0], mem_near, 1)
     cast_out = cast(2, out_hbm.at[0], w_out_near, 1)
@@ -144,7 +169,9 @@
 
     fetch_selected = pltpu.make_async_copy(selected_hbm, selected, fetch_sem.at[3])
     fetch_lengths = pltpu.make_async_copy(lengths_hbm, lengths, fetch_sem.at[4])
-    fetch_mem = pltpu.make_async_copy(memory_hbm.at[0], mem, fetch_sem.at[5])
+    fetch_mem = pltpu.make_async_copy(
+        memory_hbm.at[0, :, kv_of(0)], mem_block.at[0], fetch_sem.at[5]
+    )
     fetch_out = pltpu.make_async_copy(out_hbm.at[0], w_out, fetch_sem.at[6])
 
     @pl.when(section == 0)
@@ -200,6 +227,9 @@
         def send_one(k):
             if not sent:
                 pl.semaphore_wait(barrier, len(offsets))
+                pl.semaphore_signal(
+                    ready_sem, inc=1, device_id={"section": 1}, device_id_type=MESH
+                )
             copy = copy_to(0, k, k, part.at[k], part_in.at[0, k], block_device(k, 1))
             copy.start()
             sent.append(copy)
@@ -208,6 +238,11 @@
         cast_hidden.start()
         cast_mem.start()
         cast_out.start()
+        for k in far_first:
+            stage_memory(k).wait_recv()
+            copy = regroup(k, opposite(k))
+            copy.start()
+            sent.append(copy)
         for copy in [*sent, cast_hidden, cast_mem, cast_out]:
             copy.wait_send()
         cast_done.wait_recv()
@@ -215,6 +250,12 @@
 
     @pl.when(section == 1)
     def _():
+        pending = []
+
+        def start(copy):
+            copy.start()
+            pending.append(copy)
+
         fetch_selected.start()
         fetch_lengths.start()
         fetch_mem.start()
@@ -232,37 +273,94 @@
             hit = jnp.where(first_block * block + lane < lengths[b], hit, 0.0)
             for g in range(heads_kv):
                 live[b, g] = jnp.broadcast_to(hit[g : g + 1, :], (group, tokens))
+
+        pl.semaphore_wait(ready_sem, 1)
+        for k in far_first:
+            start(stage_memory(k))
+
+        row = lax.broadcasted_iota(jnp.int32, (len(offsets), tokens), 0)
+        row_lane = lax.broadcasted_iota(jnp.int32, (len(offsets), tokens), 1)
+        row_first = jnp.zeros((len(offsets), tokens), jnp.int32)
+        for k in range(len(offsets)):
+            bx, bz = in_block(k)
+            row_first = jnp.where(
+                row == k, (bx * z_size + base_z + bz) * blocks_local, row_first
+            )
+        for b in range(seqs):
+            chosen_ids = selected[b, pl.ds(kv_of(0), 1), :]
+            hit = jnp.zeros((len(offsets), tokens), F32)
+            for s in range(selected.shape[2]):
+                hit = jnp.where(
+                    chosen_ids[:, s : s + 1] == row_first + row_lane // block, 1.0, hit
+                )
+            hit = jnp.where(row_first * block + row_lane < lengths[b], hit, 0.0)
+            for k in range(len(offsets)):
+                live_block[b, k] = jnp.broadcast_to(hit[k : k + 1, :], (group, tokens))
         stat_lane = lax.broadcasted_iota(jnp.int32, (group, head), 1)
-        pending = []
-
-        def start(copy):
-            copy.start()
-            pending.append(copy)
-
-        def attend(layer, k, memory):
-            g = kv_of(k)
-            peaks, sums = [], []
+        def score_of(q, keys, mask):
+            score = lax.dot_general(
+                q, keys, (((1,), (1,)), ((), ())), preferred_element_type=F32
+            )
+            return jnp.where(mask, score * scale, FLOOR)
+
+        def mix(weight, values):
+            high = weight.astype(BF16)
+            low = (weight - high.astype(F32)).astype(BF16)
+            mixed = jnp.dot(
+                jnp.concatenate([high, low], axis=0), values, preferred_element_type=F32
+            )
+            return mixed[:group] + mixed[group:]
+
+        def stats_of(peaks, sums):
+            stats = jnp.where(stat_lane < 3, sums[0], sums[1])
+            stats = jnp.where(stat_lane < 2, peaks[1], stats)
+            return jnp.where(stat_lane < 1, peaks[0], stats)
+
+        def attend(layer, ks, memory):
+            pairs = [(k, b) for k in ks for b in range(seqs)]
+            heads = [kv_of(k) for k, b in pairs]
+            masks = [live[b, g] > 0.5 for (k, b), g in zip(pairs, heads)]
+            scores = [
+                score_of(query[layer, k, b], memory[b, g, :, 0].reshape(tokens, head), mask)
+                for (k, b), g, mask in zip(pairs, heads, masks)
+            ]
+            peaks = [jnp.max(score, axis=1, keepdims=True) for score in scores]
+            weights = [
+                jnp.where(mask, jnp.exp(score - peak), 0.0)
+                for score, peak, mask in zip(scores, peaks, masks)
+            ]
+            sums = [jnp.sum(weight, axis=1, keepdims=True) for weight in weights]
+            for (k, b), g, weight in zip(pairs, heads, weights):
+                local[layer, k, b] = mix(weight, memory[b, g, :, 1].reshape(tokens, head))
+            for n, k in enumerate(ks):
+                at = slice(n * seqs, (n + 1) * seqs)
+                local[layer, k, seqs] = stats_of(peaks[at], sums[at])
+
+        def attend_block(layer):
+            members = range(len(offsets))
+            outs, peaks, sums = [], [], []
             for b in range(seqs):
-                keys = memory[b, g, :, 0].reshape(tokens, head)
-                values = memory[b, g, :, 1].reshape(tokens, head)
-                mask = live[b, g] > 0.5
-                score = lax.dot_general(
-                    query[layer, k, b], keys, (((1,), (1,)), ((), ())), preferred_element_type=F32
-                )
-                score = jnp.where(mask, score * scale, FLOOR)
-                peak = jnp.max(score, axis=1, keepdims=True)
-                weight = jnp.where(mask, jnp.exp(score - peak), 0.0)
-                high = weight.astype(BF16)
-                low = (weight - high.astype(F32)).astype(BF16)
-                both = jnp.concatenate([high, low], axis=0)
-                mixed = jnp.dot(both, values, preferred_element_type=F32)
-                local[layer, k, b] = mixed[:group] + mixed[group:]
+                masks = [live_block[b, k] > 0.5 for k in members]
+                scores = [
+                    score_of(
+                        query[layer, 0, b], mem_block[k, b, :, 0].reshape(tokens, head), masks[k]
+                    )
+                    for k in members
+                ]
+                highest = scores[0]
+                for score in scores[1:]:
+                    highest = jnp.maximum(highest, score)
+                peak = jnp.max(highest, axis=1, keepdims=True)
+                out = jnp.zeros((group, head), F32)
+                total_weight = jnp.zeros((group, tokens), F32)
+                for k in members:
+                    weight = jnp.where(masks[k], jnp.exp(scores[k] - peak), 0.0)
+                    total_weight = total_weight + weight
+                    out = out + mix(weight, mem_block[k, b, :, 1].reshape(tokens, head))
+                outs.append(out)
                 peaks.append(peak)
-                sums.append(jnp.sum(weight, axis=1, keepdims=True))
-            stats = sums[1]
-            stats = jnp.where(stat_lane < 3, sums[0], stats)
-            stats = jnp.where(stat_lane < 2, peaks[1], stats)
-            local[layer, k, seqs] = jnp.where(stat_lane < 1, peaks[0], stats)
+                sums.append(jnp.sum(total_weight, axis=1, keepdims=True))
+            return outs, stats_of(peaks, sums)
 
         def combine(parts):
             top = parts[0][seqs]
@@ -279,7 +377,7 @@
                 outs = [outs[b] + p[b] * wides[b] for b in range(seqs)]
             return outs, jnp.where(stat_lane < 2, top, sums)
 
-        def after_projection(layer, value, wide_of, memory, memory_ready, weights, weights_ready):
+        def after_projection(layer, value, wide_of, memory_ready, weights, weights_ready):
             stage = 6 * layer
             total[layer] = value
             if layer == 0:
@@ -306,22 +404,29 @@
                 own_q.append(q.astype(F32))
                 own_k.append((value[seqs, b : b + 1, :] * inverse).astype(BF16).astype(F32))
                 own_v.append((value[seqs, 2 + b : 3 + b, :] * inverse).astype(BF16).astype(F32))
-            for k in far_first:
-                slot = opposite(k)
-                start(block_copy(2, k, slot, query.at[layer, 0], query.at[layer, slot]))
+            if layer == 0:
+                for k in far_first:
+                    slot = opposite(k)
+                    start(block_copy(2, k, slot, query.at[layer, 0], query.at[layer, slot]))
             own_score = [
                 jnp.sum(own_q[b] * own_k[b], axis=1, keepdims=True) * scale for b in range(seqs)
             ]
 
             memory_ready()
-            attend(layer, 0, memory)
-            for k in near_first:
-                block_copy(2, k, k, query.at[layer, 0], query.at[layer, k]).wait_recv()
-                attend(layer, k, memory)
-                start(block_copy(3, k, k, local.at[layer, k], local_in.at[layer, k]))
-            for k in near_first:
-                block_copy(3, k, k, local.at[layer, k], local_in.at[layer, k]).wait_recv()
-            outs, stats = combine([local[layer, 0], *[local_in[layer, k] for k in near_first]])
+            if layer == 0:
+                attend(layer, [0], mem_near)
+                for distance in sorted({hops[k] for k in near_first}):
+                    batch = [k for k in near_first if hops[k] == distance]
+                    for k in batch:
+                        block_copy(2, k, k, query.at[layer, 0], query.at[layer, k]).wait_recv()
+                    attend(layer, batch, mem_near)
+                    for k in batch:
+                        start(block_copy(3, k, k, local.at[layer, k], local_in.at[layer, k]))
+                for k in near_first:
+                    block_copy(3, k, k, local.at[layer, k], local_in.at[layer, k]).wait_recv()
+                outs, stats = combine([local[layer, 0], *[local_in[layer, k] for k in near_first]])
+            else:
+                outs, stats = attend_block(layer)
             for b in range(seqs):
                 merged[layer, b] = outs[b]
             merged[layer, seqs] = stats
@@ -367,7 +472,7 @@
             return hin[1].astype(F32)
 
         new = after_projection(
-            0, value, first_hidden, mem_near, cast_mem.wait_recv, w_out_near, cast_out.wait_recv
+            0, value, first_hidden, cast_mem.wait_recv, w_out_near, cast_out.wait_recv
         )
         done[:, q_width:] = new
         fetch_gain.wait()
@@ -386,7 +491,13 @@
         for k in near_first:
             copy_to(6, k, k, part.at[k], part_in.at[1, k], block_device(k, 1)).wait_recv()
             value = value + part_in[1, k]
-        new = after_projection(1, value, lambda: wide, mem, fetch_mem.wait, w_out, fetch_out.wait)
+
+        def memory_ready():
+            fetch_mem.wait()
+            for k in far_first:
+                regroup(k, k).wait_recv()
+
+        new = after_projection(1, value, lambda: wide, memory_ready, w_out, fetch_out.wait)
         result[0, :, q_width:] = new
         for copy in pending:
             copy.wait_send()
@@ -402,7 +513,7 @@
     members = x_size * PAIR_Z
     far = z_size // PAIR_Z
     tile = (seqs + 1, group, head)
-    hbm = pl.BlockSpec(memory_space=pl.ANY)
+    hbm = pl.BlockSpec(memory_space=pltpu.HBM)
     slots = max(members, far)
     result = pl.pallas_call(
         functools.partial(kernel, sizes),
@@ -417,9 +528,11 @@
             pltpu.VMEM(qkv_weight.shape[1:], BF16),
             pltpu.VMEM(out_weight.shape[1:], BF16),
             pltpu.VMEM(out_weight.shape[1:], BF16),
-            pltpu.VMEM(memory.shape[1:], BF16),
+            pltpu.VMEM((members, seqs, *memory.shape[3:]), BF16),
+            pltpu.VMEM((members, seqs, *memory.shape[3:]), BF16),
             pltpu.VMEM(memory.shape[1:], BF16),
             pltpu.VMEM((seqs, heads_kv, group, blocks_local * block), F32),
+            pltpu.VMEM((seqs, members, group, blocks_local * block), F32),
             pltpu.VMEM((members, *tile), F32),
             pltpu.VMEM((2, members, *tile), F32),
             pltpu.VMEM((2, *tile), F32),
@@ -436,10 +549,14 @@
             pltpu.VMEM((seqs, heads_total + width), BF16),
             pltpu.SemaphoreType.DMA((8 + members,)),
             pltpu.SemaphoreType.DMA((2, 4)),
+            pltpu.SemaphoreType.REGULAR,
+            pltpu.SemaphoreType.DMA((4, members)),
             pltpu.SemaphoreType.DMA((12, slots)),
             pltpu.SemaphoreType.DMA((12, slots)),
         ],
-        compiler_params=pltpu.CompilerParams(collective_id=0, has_side_effects=True),
+        compiler_params=pltpu.CompilerParams(
+            collective_id=0, has_side_effects=True, vmem_limit_bytes=VMEM_BYTES
+        ),
         name="decode",
     )(lengths, hidden_in, norm_gain, selected, qkv_weight, out_weight, memory)
     return result[:, :, heads_total:], result[:, :, :heads_total]

time: 89.5 us -> 89 us (level)
  no operation moved by 1% of the time
where the time goes in v2:
time: 89 us; the launch traced here: 88.8 us
  Pallas kernels  85.6 us (96%)
  local copies, waits for them, and re-layouts  2.53 us (3%)
    pallas_call x1, Pallas kernels, body(): pl.pallas_call(functools.partial(kernel, sizes), out_shape=jax.ShapeDtype...  85.6 us
    slice x2, local copies, waits for them, and re-layouts, body(): return (result[:, :, heads_total:], result[:, :, :heads_total])  2.53 us

profile of v2, /device:TPU:33, one launch (start us, length us, event | category | flops | bytes accessed | tf_op | source)
XLA Modules:
  0.0 88.8 jit_solution(15995007556721192636)
XLA Ops:
  0.6 85.6 %decode.1 = bf16[1,2,8320]{2,1,0:T(2,128)(2,1)} custom-call(s32[2]{0:T(128)} %lengths_hbm.1, bf16[2,128]{1,0:T(2,128)(2,1)} %hidden_hbm.1, bf16[1,128]{1,0:T(2,128)(2,1)} %gain_hbm.1, s32[2,8,16]{2,1,0:T(8,128)} %selected_hbm.1, bf16[1,128,10240]{2,1,0:T(8,128)(2,1)} %qkv_hbm.1, bf16[1,8192,128]{2,1,0:T(8,128)(2,1)} %out_hbm.1, ...), custom_call_target="tpu_custom_call" | custom-call | tf_op jit(solution)/shard_map/decode/pallas_call | solution.py:518
  86.2 1.1 %slice.6 = bf16[1,2,128]{2,1,0:T(2,128)(2,1)} slice(bf16[1,2,8320]{2,1,0:T(2,128)(2,1)} %decode.1), slice={[0:1], [0:2], [8192:8320]} | slice | bytes 1024 | tf_op jit(solution)/shard_map/slice | solution.py:562
  87.4 1.4 %slice.7 = bf16[1,2,8192]{2,1,0:T(2,128)(2,1)} slice(bf16[1,2,8320]{2,1,0:T(2,128)(2,1)} %decode.1), slice={[0:1], [0:2], [0:8192]} | slice | bytes 65536 | tf_op jit(solution)/shard_map/slice | solution.py:562

commit v3 on v2

--- a/solution.py
+++ b/solution.py
@@ -136,10 +136,10 @@
             device_id_type=MESH,
         )
 
-    def regroup(k, slot):
+    def regroup(k, slot, piece=()):
         return pltpu.make_async_remote_copy(
-            src_ref=mem_stage.at[k],
-            dst_ref=mem_block.at[slot],
+            src_ref=mem_stage.at[(k, *piece)],
+            dst_ref=mem_block.at[(slot, *piece)],
             send_sem=group_sem.at[2, k],
             recv_sem=group_sem.at[3, slot],
             device_id=block_device(k, 1),
@@ -240,9 +240,11 @@
         cast_out.start()
         for k in far_first:
             stage_memory(k).wait_recv()
-            copy = regroup(k, opposite(k))
-            copy.start()
-            sent.append(copy)
+            sent.append(regroup(k, opposite(k)))
+        for b in range(seqs):
+            for n in range(blocks_local):
+                for k in far_first:
+                    regroup(k, opposite(k), (b, n)).start()
         for copy in [*sent, cast_hidden, cast_mem, cast_out]:
             copy.wait_send()
         cast_done.wait_recv()

time: 89 us -> 82.9 us (0.931)
  Pallas kernels: 85.6 us -> 79.5 us
    pallas_call x1, Pallas kernels: 85.6 us -> 79.5 us  [body(): pl.pallas_call(functools.partial(kernel, sizes), out_shape=jax.ShapeDtype...]
where the time goes in v3:
time: 82.9 us; the launch traced here: 82.7 us
  Pallas kernels  79.5 us (96%)
  local copies, waits for them, and re-layouts  2.53 us (3%)
    pallas_call x1, Pallas kernels, body(): pl.pallas_call(functools.partial(kernel, sizes), out_shape=jax.ShapeDtype...  79.5 us
    slice x2, local copies, waits for them, and re-layouts, body(): return (result[:, :, heads_total:], result[:, :, :heads_total])  2.53 us

profile of v3, /device:TPU:33, one launch (start us, length us, event | category | flops | bytes accessed | tf_op | source)
XLA Modules:
  0.0 82.7 jit_solution(9381855733236540784)
XLA Ops:
  0.6 79.5 %decode.1 = bf16[1,2,8320]{2,1,0:T(2,128)(2,1)} custom-call(s32[2]{0:T(128)} %lengths_hbm.1, bf16[2,128]{1,0:T(2,128)(2,1)} %hidden_hbm.1, bf16[1,128]{1,0:T(2,128)(2,1)} %gain_hbm.1, s32[2,8,16]{2,1,0:T(8,128)} %selected_hbm.1, bf16[1,128,10240]{2,1,0:T(8,128)(2,1)} %qkv_hbm.1, bf16[1,8192,128]{2,1,0:T(8,128)(2,1)} %out_hbm.1, ...), custom_call_target="tpu_custom_call" | custom-call | tf_op jit(solution)/shard_map/decode/pallas_call | solution.py:520
  80.2 1.1 %slice.6 = bf16[1,2,128]{2,1,0:T(2,128)(2,1)} slice(bf16[1,2,8320]{2,1,0:T(2,128)(2,1)} %decode.1), slice={[0:1], [0:2], [8192:8320]} | slice | bytes 1024 | tf_op jit(solution)/shard_map/slice | solution.py:564
  81.3 1.4 %slice.7 = bf16[1,2,8192]{2,1,0:T(2,128)(2,1)} slice(bf16[1,2,8320]{2,1,0:T(2,128)(2,1)} %decode.1), slice={[0:1], [0:2], [0:8192]} | slice | bytes 65536 | tf_op jit(solution)/shard_map/slice | solution.py:564

commit v4 on v3

--- a/solution.py
+++ b/solution.py
@@ -199,7 +199,7 @@
 
     def project(wide, ready, send_one):
         normed = (wide * gain[...].astype(F32)).astype(BF16)
-        squares = wide * wide
+        squares = jnp.broadcast_to(jnp.sum(wide * wide, axis=1, keepdims=True), wide.shape)
         for k in [*far_first, 0]:
             g = kv_of(k)
             at_k = pl.multiple_of(q_width + g * head, head)
@@ -243,8 +243,9 @@
             sent.append(regroup(k, opposite(k)))
         for b in range(seqs):
             for n in range(blocks_local):
-                for k in far_first:
-                    regroup(k, opposite(k), (b, n)).start()
+                for half in range(2):
+                    for k in far_first:
+                        regroup(k, opposite(k), (b, n, half)).start()
         for copy in [*sent, cast_hidden, cast_mem, cast_out]:
             copy.wait_send()
         cast_done.wait_recv()
@@ -399,7 +400,7 @@
 
             own_q, own_k, own_v = [], [], []
             for b in range(seqs):
-                mean = jnp.sum(value[seqs, 4 + b : 5 + b, :], axis=1, keepdims=True) / model_width
+                mean = value[seqs, 4 + b : 5 + b, :] / model_width
                 inverse = lax.rsqrt(mean + EPSILON)
                 q = (value[b] * inverse).astype(BF16)
                 query[layer, 0, b] = q
@@ -503,6 +504,18 @@
         result[0, :, q_width:] = new
         for copy in pending:
             copy.wait_send()
+
+
+def hand_out(heads_total, result, hidden_out, attention_out, held, sem):
+    fetch = pltpu.make_async_copy(result, held, sem.at[2])
+    attention = pltpu.make_async_copy(held.at[:, :, :heads_total], attention_out, sem.at[0])
+    hidden = pltpu.make_async_copy(held.at[:, :, heads_total:], hidden_out, sem.at[1])
+    fetch.start()
+    fetch.wait()
+    attention.start()
+    hidden.start()
+    attention.wait()
+    hidden.wait()
 
 
 def body(hidden_in, norm_gain, qkv_weight, out_weight, memory, lengths, selected):
@@ -561,7 +574,17 @@
         ),
         name="decode",
     )(lengths, hidden_in, norm_gain, selected, qkv_weight, out_weight, memory)
-    return result[:, :, heads_total:], result[:, :, :heads_total]
+    return pl.pallas_call(
+        functools.partial(hand_out, heads_total),
+        out_shape=(
+            jax.ShapeDtypeStruct((1, seqs, width), BF16),
+            jax.ShapeDtypeStruct((1, seqs, heads_total), BF16),
+        ),
+        in_specs=[hbm],
+        out_specs=(hbm, hbm),
+        scratch_shapes=[pltpu.VMEM(result.shape, BF16), pltpu.SemaphoreType.DMA((3,))],
+        name="hand_out",
+    )(result)
 
 
 def solution(mesh):

time: 82.9 us -> 80.7 us (0.973)
  local copies, waits for them, and re-layouts: 2.53 us -> 0 us
    slice x2 -> x0, local copies, waits for them, and re-layouts: 2.53 us -> none  [body(): return (result[:, :, heads_total:], result[:, :, :heads_total])]
    pallas_call x0 -> x1, Pallas kernels: none -> 1.4 us  [body(): pl.pallas_call(functools.partial(hand_out, heads_total), out_shape=(jax.S...]
    pallas_call x1, Pallas kernels: 79.5 us -> 78.5 us  [body(): pl.pallas_call(functools.partial(kernel, sizes), out_shape=jax.ShapeDtype...]
where the time goes in v4:
time: 80.7 us; the launch traced here: 80.5 us
  Pallas kernels  79.9 us (99%)
    pallas_call x1, Pallas kernels, body(): pl.pallas_call(functools.partial(kernel, sizes), out_shape=jax.ShapeDtype...  78.5 us

profile of v4, /device:TPU:33, one launch (start us, length us, event | category | flops | bytes accessed | tf_op | source)
XLA Modules:
  0.0 80.5 jit_solution(11461096367633511582)
XLA Ops:
  0.6 78.5 %decode.1.result = bf16[1,2,8320]{2,1,0:T(2,128)(2,1)} custom-call(s32[2]{0:T(128)} %lengths_hbm.1, bf16[2,128]{1,0:T(2,128)(2,1)} %hidden_hbm.1, bf16[1,128]{1,0:T(2,128)(2,1)} %gain_hbm.1, s32[2,8,16]{2,1,0:T(8,128)} %selected_hbm.1, bf16[1,128,10240]{2,1,0:T(8,128)(2,1)} %qkv_hbm.1, bf16[1,8192,128]{2,1,0:T(8,128)(2,1)} %out_hbm.1, ...), custom_call_target="tpu_custom_call" | custom-call | tf_op jit(solution)/shard_map/decode/pallas_call | solution.py:533
  79.1 1.4 %hand_out.1 = (bf16[1,2,128]{2,1,0:T(2,128)(2,1)}, bf16[1,2,8192]{2,1,0:T(2,128)(2,1)}) custom-call(bf16[1,2,8320]{2,1,0:T(2,128)(2,1)} %decode.1.result), custom_call_target="tpu_custom_call" | custom-call | tf_op jit(solution)/shard_map/hand_out/pallas_call | solution.py:577

commit v5 on v4

--- a/solution.py
+++ b/solution.py
@@ -200,14 +200,18 @@
     def project(wide, ready, send_one):
         normed = (wide * gain[...].astype(F32)).astype(BF16)
         squares = jnp.broadcast_to(jnp.sum(wide * wide, axis=1, keepdims=True), wide.shape)
-        for k in [*far_first, 0]:
+        order = [*far_first, 0]
+
+        def multiply(k):
             g = kv_of(k)
             at_k = pl.multiple_of(q_width + g * head, head)
             at_v = pl.multiple_of(q_width + kv_width + g * head, head)
             ready(k)
-            qs = jnp.dot(normed, w_in[:, q_columns(k)], preferred_element_type=F32)
-            ks = jnp.dot(normed, w_in[:, pl.ds(at_k, head)], preferred_element_type=F32)
-            vs = jnp.dot(normed, w_in[:, pl.ds(at_v, head)], preferred_element_type=F32)
+            columns = [q_columns(k), pl.ds(at_k, head), pl.ds(at_v, head)]
+            return [jnp.dot(normed, w_in[:, at], preferred_element_type=F32) for at in columns]
+
+        for k in order:
+            qs, ks, vs = multiply(k)
             for b in range(seqs):
                 for r in range(group):
                     part[k, b, r : r + 1, :] = qs[b : b + 1, r * head : (r + 1) * head]
@@ -241,11 +245,20 @@
         for k in far_first:
             stage_memory(k).wait_recv()
             sent.append(regroup(k, opposite(k)))
-        for b in range(seqs):
-            for n in range(blocks_local):
-                for half in range(2):
-                    for k in far_first:
-                        regroup(k, opposite(k), (b, n, half)).start()
+        piece = block // 4
+
+        def start_piece(ks, n, carry):
+            b = n // (blocks_local * 2 * 4)
+            j = lax.rem(n // (2 * 4), blocks_local)
+            half = lax.rem(n // 4, 2)
+            at = pl.ds(pl.multiple_of(lax.rem(n, 4) * piece, piece), piece)
+            for k in ks:
+                regroup(k, opposite(k), (b, j, half, at)).start()
+            return carry
+
+        for dz in (1, 0):
+            ks = [k for k in far_first if offsets[k][1] == dz]
+            lax.fori_loop(0, seqs * blocks_local * 2 * 4, functools.partial(start_piece, ks), 0)
         for copy in [*sent, cast_hidden, cast_mem, cast_out]:
             copy.wait_send()
         cast_done.wait_recv()

time: 80.7 us -> 80.3 us (level)
  no operation moved by 1% of the time
where the time goes in v5:
time: 80.3 us; the launch traced here: 80.1 us
  Pallas kernels  79.4 us (99%)
    pallas_call x1, Pallas kernels, body(): pl.pallas_call(functools.partial(kernel, sizes), out_shape=jax.ShapeDtype...  78 us

profile of v5, /device:TPU:33, one launch (start us, length us, event | category | flops | bytes accessed | tf_op | source)
XLA Modules:
  0.0 80.1 jit_solution(15672492979628316027)
XLA Ops:
  0.6 78.0 %decode.1.result = bf16[1,2,8320]{2,1,0:T(2,128)(2,1)} custom-call(s32[2]{0:T(128)} %lengths_hbm.1, bf16[2,128]{1,0:T(2,128)(2,1)} %hidden_hbm.1, bf16[1,128]{1,0:T(2,128)(2,1)} %gain_hbm.1, s32[2,8,16]{2,1,0:T(8,128)} %selected_hbm.1, bf16[1,128,10240]{2,1,0:T(8,128)(2,1)} %qkv_hbm.1, bf16[1,8192,128]{2,1,0:T(8,128)(2,1)} %out_hbm.1, ...), custom_call_target="tpu_custom_call" | custom-call | tf_op jit(solution)/shard_map/decode/pallas_call | solution.py:546
  78.7 1.4 %hand_out.1 = (bf16[1,2,128]{2,1,0:T(2,128)(2,1)}, bf16[1,2,8192]{2,1,0:T(2,128)(2,1)}) custom-call(bf16[1,2,8320]{2,1,0:T(2,128)(2,1)} %decode.1.result), custom_call_target="tpu_custom_call" | custom-call | tf_op jit(solution)/shard_map/hand_out/pallas_call | solution.py:590

commit v6 on v5

--- a/solution.py
+++ b/solution.py
@@ -431,8 +431,8 @@
             memory_ready()
             if layer == 0:
                 attend(layer, [0], mem_near)
-                for distance in sorted({hops[k] for k in near_first}):
-                    batch = [k for k in near_first if hops[k] == distance]
+                for close in (True, False):
+                    batch = [k for k in near_first if (hops[k] == 1) == close]
                     for k in batch:
                         block_copy(2, k, k, query.at[layer, 0], query.at[layer, k]).wait_recv()
                     attend(layer, batch, mem_near)

time: 80.3 us -> 80.4 us (level)
  no operation moved by 1% of the time
where the time goes in v6:
time: 80.4 us; the launch traced here: 80.2 us
  Pallas kernels  79.6 us (99%)
    pallas_call x1, Pallas kernels, body(): pl.pallas_call(functools.partial(kernel, sizes), out_shape=jax.ShapeDtype...  78.2 us

profile of v6, /device:TPU:33, one launch (start us, length us, event | category | flops | bytes accessed | tf_op | source)
XLA Modules:
  0.0 80.2 jit_solution(10162676667217616058)
XLA Ops:
  0.6 78.2 %decode.1.result = bf16[1,2,8320]{2,1,0:T(2,128)(2,1)} custom-call(s32[2]{0:T(128)} %lengths_hbm.1, bf16[2,128]{1,0:T(2,128)(2,1)} %hidden_hbm.1, bf16[1,128]{1,0:T(2,128)(2,1)} %gain_hbm.1, s32[2,8,16]{2,1,0:T(8,128)} %selected_hbm.1, bf16[1,128,10240]{2,1,0:T(8,128)(2,1)} %qkv_hbm.1, bf16[1,8192,128]{2,1,0:T(8,128)(2,1)} %out_hbm.1, ...), custom_call_target="tpu_custom_call" | custom-call | tf_op jit(solution)/shard_map/decode/pallas_call | solution.py:546
  78.8 1.4 %hand_out.1 = (bf16[1,2,128]{2,1,0:T(2,128)(2,1)}, bf16[1,2,8192]{2,1,0:T(2,128)(2,1)}) custom-call(bf16[1,2,8320]{2,1,0:T(2,128)(2,1)} %decode.1.result), custom_call_target="tpu_custom_call" | custom-call | tf_op jit(solution)/shard_map/hand_out/pallas_call | solution.py:590
